TPU v7x, 256 devices: a whole 4x4x8 slice. The times are simulated.
256 devices in a mesh: seq: 32 (over z, y), vocab: 8 (over x, core).
Axes of the slice: x: 4, y: 4, z: 8, core: 2. Of those that a mesh axis runs over, the one named last changes fastest.
Arguments:
- hidden: bfloat16 [3072, 3584], P('seq', 'vocab'), may hold values from -40 to 40
- lm_head: bfloat16 [3584, 152064], P(None, ('seq', 'vocab')), may hold values from -1 to 1
- positions: int32 [3072], replicated, may hold values from 0 to 3071, as said below
- vocab_limits: int32 [3072], replicated, may hold values from 76032 to 152064
- loss_mask: int32 [3072], P('seq'), may hold values 0 or 1
Outputs:
- token_entropy: float32 [3072], P('seq')
- mean_entropy: float32 [], replicated
Inputs may be any that keep to these rules, and one draw needn't show every extreme that they name: A permutation of the positions 0 to 3071: the response is cut into 64 blocks of 48 consecutive positions; rows i * 96 to i * 96 + 96 // 2 - 1 hold the positions of block i, the next 48 rows those of block 63 - i, in any order within a block.
All inputs are finite; a program needn't handle non-finite values. No bound on the sum of `loss_mask` on one device may be relied on, other than what follows from the above.
Results may differ from a plain program's by a relative error of at most 0.0003.
Values may be sent and summed in bfloat16 or wider, within the bound.
A program may use at most 128 MiB of HBM per device.

v0:
```python
import jax
import jax.numpy as jnp
from jax import lax
from jax.sharding import Mesh
from jax.sharding import PartitionSpec as P

SEQ_VOCAB = ("seq_0", "seq_1", "vocab_0", "vocab_1")
SEQ = ("seq_0", "seq_1")
VOCAB = ("vocab_0", "vocab_1")
masked_value = -1e30


def gather_axes(shard, axes, dim):
    whole = shard
    for number in range(len(axes) - 1, -1, -1):
        whole = lax.all_gather(whole, axes[number], axis=dim, tiled=True)
    return whole


def gathered_once(shard, axis):
    leaves = jax.tree.leaves(shard)
    order = sorted(range(len(leaves)), key=lambda k: -leaves[k].size)
    width = (1, *leaves[order[0]].shape)[-1]
    lines = [
        jnp.pad(leaves[k].reshape(-1), (0, -leaves[k].size % width)).reshape(-1, width)
        for k in order
    ]
    both, at, found = (lax.all_gather(jnp.concatenate(lines), axis), 0, {})
    for k, line in zip(order, lines):
        section = both[:, at : at + len(line)].reshape(len(both), -1)
        found[k] = section[:, : leaves[k].size].reshape(-1, *leaves[k].shape)
        at += len(line)
    numbers = iter(range(len(leaves)))
    return jax.tree.map(lambda _: found[next(numbers)], shard)


def combined_by_axis(shard, axes, combine):
    for axis in axes:
        pieces = gathered_once(shard, axis)
        shard = jax.tree.map(lambda part: part[0], pieces)
        for k in range(1, lax.axis_size(axis)):
            shard = combine(shard, jax.tree.map(lambda part: part[k], pieces))
    return shard


def copy_for_each(shard, axis):
    copies = jnp.broadcast_to(shard, (lax.axis_size(axis), *shard.shape))
    return lax.all_to_all(copies, axis, split_axis=0, concat_axis=0, tiled=True)


def taken_together(shard, axis):
    everything = copy_for_each(shard, axis)
    return jnp.sum(everything, axis=0)


def together(arrays, axis):
    flat, at, finished = (jnp.concatenate([a.reshape(-1) for a in arrays]), 0, [])
    total = taken_together(flat, axis)
    for a in arrays:
        finished.append(total[at : at + a.size].reshape(a.shape))
        at += a.size
    return tuple(finished)


def row_stats(logits, row_limits, first_column):
    columns = first_column + lax.iota(jnp.int32, logits.shape[1])
    allowed = columns[None, :] < row_limits[:, None]
    row_peak = jnp.max(jnp.where(allowed, logits, masked_value), axis=1)
    shifted = logits - row_peak[:, None]
    weights = jnp.where(allowed, jnp.exp(shifted), 0.0)
    row_total = jnp.sum(weights, axis=1)
    row_moment = jnp.sum(weights * jnp.where(allowed, shifted, 0.0), axis=1)
    return (row_peak, row_total, row_moment)


def combine_stats(first, second):
    peak_one, total_one, moment_one = first
    peak_two, total_two, moment_two = second
    shared = jnp.maximum(peak_one, peak_two)
    ratio_one = jnp.exp(peak_one - shared)
    ratio_two = jnp.exp(peak_two - shared)
    total = ratio_one * total_one + ratio_two * total_two
    moment = ratio_one * (moment_one + total_one * (peak_one - shared)) + ratio_two * (
        moment_two + total_two * (peak_two - shared)
    )
    return (shared, total, moment)


def local(hidden, lm_head, positions, vocab_limits, loss_mask):
    tok_dev = hidden.shape[0]
    width_dev = lm_head.shape[1]
    tokens_all = positions.shape[0]
    first_column = lax.axis_index(SEQ_VOCAB) * width_dev
    all_tokens = gather_axes(hidden, SEQ, 0)
    logits = jnp.dot(
        lax.all_gather(all_tokens, VOCAB, axis=1, tiled=True),
        lm_head,
        preferred_element_type=jnp.float32,
    )
    stats = row_stats(logits, vocab_limits, first_column)
    own_start = lax.axis_index(SEQ) * tok_dev
    row_peak, row_total, row_moment = combined_by_axis(stats, SEQ_VOCAB, combine_stats)
    entropy_rows = jnp.log(row_total) - row_moment / row_total
    arranged = jnp.zeros((tokens_all,), jnp.float32).at[positions].set(entropy_rows)
    token_entropy = lax.dynamic_slice_in_dim(arranged, own_start, tok_dev)
    mask_float = loss_mask.astype(jnp.float32)
    masked_sum, mask_count = together(
        (jnp.sum(token_entropy * mask_float), jnp.sum(mask_float)), SEQ
    )
    mean_entropy = masked_sum / jnp.maximum(mask_count, 1.0)
    return (token_entropy, mean_entropy)


def solution(mesh):
    torus = Mesh(mesh.devices.reshape(8, 4, 4, 2), ("seq_0", "seq_1", "vocab_0", "vocab_1"))
    in_specs = (P(SEQ, VOCAB), P(None, SEQ_VOCAB), P(), P(), P(SEQ))
    out_specs = (P(SEQ), P())
    return jax.shard_map(local, mesh=torus, in_specs=in_specs, out_specs=out_specs, check_vma=False)
```

profile of v0, /device:TPU:1, one launch (start us, length us, event | category | flops | bytes accessed | tf_op | source)
XLA Modules:
  0.0 298.8 jit_solution(5486878715596462331)
XLA Ops:
  7.2 0.0 copy-start.1
  7.2 0.0 copy-start
  7.2 0.0 all-gather.11.cloned.1.call-start
  7.2 13.0 %all_gather.33 = bf16[384,448]{1,0:T(8,128)(2,1)} all-gather(bf16[96,448]{1,0:T(8,128)(2,1)} %param.5), channel_id=1, replica_groups=mesh['seq_0'=8,'seq_1'=4,'vocab_0'=4,'vocab_1'=2] {'seq_1'}, dimensions={0}, use_global_device_ids=true | all-gather | bytes 430080 | tf_op jit(solution)/shard_map/all_gather | solution.py:16
  20.2 0.0 all-gather.11.cloned.1.call-update
  20.3 0.0 all-gather.13.cloned.1.call-start
  20.3 48.6 %all-gather.11.cloned.1.call-done = bf16[3072,448]{1,0:T(8,128)(2,1)} async-done(((bf16[384,448]{1,0:T(8,128)(2,1)}), bf16[3072,448]{1,0:T(8,128)(2,1)}) %all-gather.11.cloned.1.call-update) | async-done | bytes 2752528 | tf_op jit(solution)/shard_map/all_gather | solution.py:16
  68.9 4.6 %copy.10 = bf16[3072,448]{0,1:T(8,128)(2,1)} copy(bf16[3072,448]{1,0:T(8,128)(2,1)} %all-gather.11.cloned.1.call-done) | data formatting | bytes 5505024 | tf_op jit(solution)/shard_map/all_gather | solution.py:16
  73.5 0.0 all-gather.13.cloned.1.call-update
  73.6 0.0 copy-done.1
  73.6 109.1 %all-gather.13.cloned.1.call-done = bf16[3072,3584]{0,1:T(8,128)(2,1)} async-done(((bf16[3072,448]{0,1:T(8,128)(2,1)}), bf16[3072,3584]{0,1:T(8,128)(2,1)}) %all-gather.13.cloned.1.call-update) | async-done | bytes 22020112 | tf_op jit(solution)/shard_map/all_gather | solution.py:96
  182.8 0.0 copy-done
  182.8 18.4 %fusion = (f32[3072]{0:T(1024)S(1)}, f32[3072,594]{0,1:T(8,128)S(1)}) fusion(s32[3072]{0:T(1024)S(1)} %copy-done, s32[594]{0:T(1024)S(1)} %iota_add_fusion, bf16[3072,3584]{0,1:T(8,128)(2,1)} %all-gather.13.cloned.1.call-done, bf16[3584,594]{0,1:T(8,128)(2,1)} %param.6), kind=kOutput, calls=%fused_computation.4 | convolution fusion | flops 13085408256 | bytes 33603912 | tf_op jit(solution)/shard_map/dot_general | solution.py:95
  201.2 0.0 copy-start.2
  201.2 2.5 fusion.3
  203.8 20.1 %all-gather.4 = f32[8,3,3072]{2,1,0:T(4,128)S(1)} all-gather(f32[1,3,3072]{2,1,0:T(4,128)S(1)} %maximum_bitcast_fusion), channel_id=2, replica_groups=mesh['seq_0'=8,'seq_1'=4,'vocab_0'=4,'vocab_1'=2] {'seq_0'}, dimensions={0}, use_global_device_ids=true | all-gather | bytes 331776 | tf_op jit(solution)/shard_map/all_gather | solution.py:28
  223.9 0.1 fusion.63
  224.0 0.3 multiply_add_fusion.6
  224.3 0.5 fusion.28
  224.8 9.9 %all-gather.5 = f32[4,3,3072]{2,1,0:T(4,128)S(1)} all-gather(f32[1,3,3072]{2,1,0:T(4,128)S(1)} %maximum_bitcast_fusion.1), channel_id=3, replica_groups=mesh['seq_0'=8,'seq_1'=4,'vocab_0'=4,'vocab_1'=2] {'seq_1'}, dimensions={0}, use_global_device_ids=true | all-gather | bytes 184320 | tf_op jit(solution)/shard_map/all_gather | solution.py:28
  234.6 0.1 fusion.70
  234.8 0.2 fusion.17
  235.0 9.2 %all-gather.6 = f32[4,3,3072]{2,1,0:T(4,128)S(1)} all-gather(f32[1,3,3072]{2,1,0:T(4,128)S(1)} %maximum_bitcast_fusion.2), channel_id=4, replica_groups=mesh['seq_0'=8,'seq_1'=4,'vocab_0'=4,'vocab_1'=2] {'vocab_0'}, dimensions={0}, use_global_device_ids=true | all-gather | bytes 184320 | tf_op jit(solution)/shard_map/all_gather | solution.py:28
  244.3 0.1 fusion.77
  244.4 0.2 fusion.6
  244.7 13.7 %all-gather.7 = f32[2,3,3072]{2,1,0:T(4,128)S(1)} all-gather(f32[1,3,3072]{2,1,0:T(4,128)S(1)} %maximum_bitcast_fusion.3), channel_id=5, replica_groups=mesh['seq_0'=8,'seq_1'=4,'vocab_0'=4,'vocab_1'=2] {'vocab_1'}, dimensions={0}, use_global_device_ids=true | all-gather | bytes 110592 | tf_op jit(solution)/shard_map/all_gather | solution.py:28
  258.4 0.1 fusion.82
  258.5 11.8 %scatter_custom_fusion = f32[3072]{0:T(1024)S(1)} fusion(s32[3072]{0:T(1024)S(1)} %compare_select_fusion.3, f32[3072]{0:T(1024)S(1)} %divide_subtract_fusion, f32[]{:T(128)} %constant.16.clone.1), kind=kCustom, calls=%fused_computation.151 | custom fusion | bytes 12292 | tf_op jit(solution)/shard_map/scatter | solution.py:104
  270.3 0.0 copy-done.2
  270.3 1.3 multiply_reduce_fusion
  271.5 1.4 pad_maximum_fusion
  273.0 15.9 %all_to_all.6 = f32[32,1,2]{2,1,0:T(1,128)S(1)} all-to-all(f32[32,1,2]{2,1,0:T(1,128)S(1)} %broadcast_in_dim.24), channel_id=1, replica_groups=mesh['seq_0'=8,'seq_1'=4,'vocab_0'=4,'vocab_1'=2] {'seq_0','seq_1'}, dimensions={0} | all-to-all | bytes 512 | tf_op jit(solution)/shard_map/all_to_all | solution.py:48
  288.8 0.1 reduce_sum.49
  288.9 0.6 fusion.83
  (8 shorter events, 0.2 us)
Async XLA Ops:
  7.2 66.4 %copy-start.1 = (s32[3072]{0:T(1024)S(1)}, s32[3072]{0:T(1024)}, u32[]{:S(2)}) copy-start(s32[3072]{0:T(1024)} %param.7) | copy-start | bytes 36868
  7.2 175.6 %copy-start = (s32[3072]{0:T(1024)S(1)}, s32[3072]{0:T(1024)}, u32[]{:S(2)}) copy-start(s32[3072]{0:T(1024)} %param.8) | copy-start | bytes 36868
  7.2 61.7 %all-gather.11.cloned.1.call-start = ((), (), s32[]{:S(2)}) async-start(), calls=%async_computation.1 | async-start | bytes 3538944 | tf_op jit(solution)/shard_map/all_gather | solution.py:16
  20.3 162.5 %all-gather.13.cloned.1.call-start = ((), (), s32[]{:S(2)}) async-start(), calls=%async_computation.2 | async-start | bytes 24772608 | tf_op jit(solution)/shard_map/all_gather | solution.py:96
  201.2 69.1 %copy-start.2 = (s32[96]{0:T(128)S(1)}, s32[96]{0:T(128)}, u32[]{:S(2)}) copy-start(s32[96]{0:T(128)} %param.9) | copy-start | bytes 1156
Sparse Core Ops, SparseCore 0:
  20.4 48.4 all-gather.10
  73.7 109.0 all-gather.12
where the time goes:
time: 299 us
  waiting for transfers between devices  158 us (53%)
  blocking collectives  81.8 us (27%)
  matrix products  18.4 us (6%)
  local copies, waits for them, and re-layouts  17.1 us (6%)
  between operations  16.7 us (6%)
  other arithmetic  6.95 us (2%)
    all_gather x1, waiting for transfers between devices, local(): lax.all_gather(all_tokens, VOCAB, axis=1, tiled=True)  109 us
    all_gather x4, blocking collectives, gathered_once(): both, at, found = (lax.all_gather(jnp.concatenate(lines), axis), 0, {})  53 us
    all_gather x1, waiting for transfers between devices, gather_axes(): whole = lax.all_gather(whole, axes[number], axis=dim, tiled=True)  48.6 us
    dot_general x1, matrix products, local(): jnp.dot(lax.all_gather(all_tokens, VOCAB, axis=1, tiled=True), lm_head, p...  18.4 us
    all_to_all x1, blocking collectives, copy_for_each(): return lax.all_to_all(copies, axis, split_axis=0, concat_axis=0, tiled=True)  15.9 us
    all_gather x1, blocking collectives, gather_axes(): whole = lax.all_gather(whole, axes[number], axis=dim, tiled=True)  13 us
    scatter x1, local copies, waits for them, and re-layouts, local(): jnp.zeros((tokens_all,), jnp.float32).at[positions].set(entropy_rows)  11.8 us
  transfers between devices with their start and end apart: 2, of which 2 were waited for; matrix products, arithmetic and copies ran while one was open for 0% of the time, Pallas kernels for 0%

commit v1 on v0

--- a/solution.py
+++ b/solution.py
@@ -93,7 +93,9 @@
     first_column = lax.axis_index(SEQ_VOCAB) * width_dev
     all_tokens = gather_axes(hidden, SEQ, 0)
     logits = jnp.dot(
-        lax.all_gather(all_tokens, VOCAB, axis=1, tiled=True),
+        jnp.concatenate(
+            lax.all_to_all(jnp.stack([all_tokens] * lax.axis_size(VOCAB)), VOCAB, 0, 0), axis=1
+        ),
         lm_head,
         preferred_element_type=jnp.float32,
     )

time: 299 us -> 442 us (1.48)
  waiting for transfers between devices: 158 us -> 288 us
  starting transfers between devices: 0.08 us -> 7.48 us
  local copies, waits for them, and re-layouts: 17.1 us -> 23.3 us
    all_to_all x0 -> x1, waiting for transfers between devices: none -> 240 us  [local(): lax.all_to_all(jnp.stack([all_tokens] * lax.axis_size(VOCAB)), VOCAB, 0, 0)]
    all_gather x1 -> x0, waiting for transfers between devices: 109 us -> none  [local(): lax.all_gather(all_tokens, VOCAB, axis=1, tiled=True)]
    another operation x0 -> x1, local copies, waits for them, and re-layouts: none -> 7.72 us  [local(): jnp.stack([all_tokens] * lax.axis_size(VOCAB))]
    all_to_all x0 -> x1, starting transfers between devices: none -> 7.44 us  [local(): lax.all_to_all(jnp.stack([all_tokens] * lax.axis_size(VOCAB)), VOCAB, 0, 0)]
where the time goes in v1:
time: 442 us
  waiting for transfers between devices  288 us (65%)
  blocking collectives  80 us (18%)
  local copies, waits for them, and re-layouts  23.3 us (5%)
  matrix products  18.8 us (4%)
  between operations  16.6 us (4%)
  starting transfers between devices  7.48 us (2%)
  other arithmetic  6.95 us (2%)
    all_to_all x1, waiting for transfers between devices, local(): lax.all_to_all(jnp.stack([all_tokens] * lax.axis_size(VOCAB)), VOCAB, 0, 0)  240 us
    all_gather x4, blocking collectives, gathered_once(): both, at, found = (lax.all_gather(jnp.concatenate(lines), axis), 0, {})  52.2 us
    all_gather x1, waiting for transfers between devices, gather_axes(): whole = lax.all_gather(whole, axes[number], axis=dim, tiled=True)  48.7 us
    dot_general x1, matrix products, local(): jnp.dot(jnp.concatenate(lax.all_to_all(jnp.stack([all_tokens] * lax.axis_...  18.8 us
    all_to_all x1, blocking collectives, copy_for_each(): return lax.all_to_all(copies, axis, split_axis=0, concat_axis=0, tiled=True)  14.9 us
    all_gather x1, blocking collectives, gather_axes(): whole = lax.all_gather(whole, axes[number], axis=dim, tiled=True)  13 us
    scatter x1, local copies, waits for them, and re-layouts, local(): jnp.zeros((tokens_all,), jnp.float32).at[positions].set(entropy_rows)  11.8 us
  transfers between devices with their start and end apart: 2, of which 2 were waited for; matrix products, arithmetic and copies ran while one was open for 0% of the time, Pallas kernels for 0%

profile of v1, /device:TPU:1, one launch (start us, length us, event | category | flops | bytes accessed | tf_op | source)
XLA Modules:
  0.0 441.6 jit_solution(15966979080843063210)
XLA Ops:
  7.2 0.0 all-gather.10.cloned.1.call-start
  7.2 13.0 %all_gather.30 = bf16[384,448]{1,0:T(8,128)(2,1)} all-gather(bf16[96,448]{1,0:T(8,128)(2,1)} %param.5), channel_id=1, replica_groups=mesh['seq_0'=8,'seq_1'=4,'vocab_0'=4,'vocab_1'=2] {'seq_1'}, dimensions={0}, use_global_device_ids=true | all-gather | bytes 430080 | tf_op jit(solution)/shard_map/all_gather | solution.py:16
  20.2 0.0 all-gather.10.cloned.1.call-update
  20.2 48.7 %all-gather.10.cloned.1.call-done = bf16[3072,448]{1,0:T(8,128)(2,1)} async-done(((bf16[384,448]{1,0:T(8,128)(2,1)}), bf16[3072,448]{1,0:T(8,128)(2,1)}) %all-gather.10.cloned.1.call-update) | async-done | bytes 2752528 | tf_op jit(solution)/shard_map/all_gather | solution.py:16
  68.9 3.1 copy.10
  72.0 7.7 %stack.2 = bf16[8,3072,448]{1,2,0:T(8,128)(2,1)} broadcast(bf16[3072,448]{0,1:T(8,128)(2,1)S(1)} %copy.10), dimensions={1,2} | broadcast | bytes 24772608 | tf_op jit(solution)/shard_map/stack | solution.py:97
  79.7 0.0 copy-start.1
  79.7 0.0 copy-start
  79.7 7.4 %all-to-all-start = ((bf16[8,3072,448]{1,2,0:T(8,128)(2,1)}), bf16[8,3072,448]{1,2,0:T(8,128)(2,1)}, u32[]{:S(2)}, u32[]{:S(2)}) async-start(bf16[8,3072,448]{1,2,0:T(8,128)(2,1)} %stack.2), calls=%async_computation | async-start | bytes 44040192 | tf_op jit(solution)/shard_map/all_to_all | solution.py:97
  87.2 0.0 copy-done.1
  87.2 239.8 %all-to-all-done = bf16[8,3072,448]{1,2,0:T(8,128)(2,1)} async-done(((bf16[8,3072,448]{1,2,0:T(8,128)(2,1)}), bf16[8,3072,448]{1,2,0:T(8,128)(2,1)}, u32[]{:S(2)}, u32[]{:S(2)}) %all-to-all-start) | async-done | bytes 22020128 | tf_op jit(solution)/shard_map/all_to_all | solution.py:97
  327.0 0.0 copy-done
  327.0 18.8 %fusion = (f32[3072]{0:T(1024)S(1)}, f32[3072,594]{0,1:T(8,128)S(1)}) fusion(s32[3072]{0:T(1024)S(1)} %copy-done, s32[594]{0:T(1024)S(1)} %iota_add_fusion, bf16[3072,3584]{0,1:T(8,128)(2,1)} %bitcast.1, bf16[3584,594]{0,1:T(8,128)(2,1)} %param.6), kind=kOutput, calls=%fused_computation.4 | convolution fusion | flops 13085408256 | bytes 33603912 | tf_op jit(solution)/shard_map/dot_general | solution.py:95
  345.8 0.0 copy-start.2
  345.8 2.6 fusion.3
  348.4 19.0 %all-gather.4 = f32[8,3,3072]{2,1,0:T(4,128)S(1)} all-gather(f32[1,3,3072]{2,1,0:T(4,128)S(1)} %maximum_bitcast_fusion), channel_id=2, replica_groups=mesh['seq_0'=8,'seq_1'=4,'vocab_0'=4,'vocab_1'=2] {'seq_0'}, dimensions={0}, use_global_device_ids=true | all-gather | bytes 331776 | tf_op jit(solution)/shard_map/all_gather | solution.py:28
  367.4 0.1 fusion.63
  367.5 0.3 multiply_add_fusion.6
  367.7 0.5 fusion.28
  368.3 9.6 %all-gather.5 = f32[4,3,3072]{2,1,0:T(4,128)S(1)} all-gather(f32[1,3,3072]{2,1,0:T(4,128)S(1)} %maximum_bitcast_fusion.1), channel_id=3, replica_groups=mesh['seq_0'=8,'seq_1'=4,'vocab_0'=4,'vocab_1'=2] {'seq_1'}, dimensions={0}, use_global_device_ids=true | all-gather | bytes 184320 | tf_op jit(solution)/shard_map/all_gather | solution.py:28
  377.8 0.1 fusion.70
  378.0 0.2 fusion.17
  378.2 9.2 %all-gather.6 = f32[4,3,3072]{2,1,0:T(4,128)S(1)} all-gather(f32[1,3,3072]{2,1,0:T(4,128)S(1)} %maximum_bitcast_fusion.2), channel_id=4, replica_groups=mesh['seq_0'=8,'seq_1'=4,'vocab_0'=4,'vocab_1'=2] {'vocab_0'}, dimensions={0}, use_global_device_ids=true | all-gather | bytes 184320 | tf_op jit(solution)/shard_map/all_gather | solution.py:28
  387.5 0.1 fusion.77
  387.6 0.2 fusion.6
  387.9 14.3 %all-gather.7 = f32[2,3,3072]{2,1,0:T(4,128)S(1)} all-gather(f32[1,3,3072]{2,1,0:T(4,128)S(1)} %maximum_bitcast_fusion.3), channel_id=5, replica_groups=mesh['seq_0'=8,'seq_1'=4,'vocab_0'=4,'vocab_1'=2] {'vocab_1'}, dimensions={0}, use_global_device_ids=true | all-gather | bytes 110592 | tf_op jit(solution)/shard_map/all_gather | solution.py:28
  402.2 0.1 fusion.82
  402.3 11.8 %scatter_custom_fusion = f32[3072]{0:T(1024)S(1)} fusion(s32[3072]{0:T(1024)S(1)} %compare_select_fusion.3, f32[3072]{0:T(1024)S(1)} %divide_subtract_fusion, f32[]{:T(128)} %constant.16.clone.1), kind=kCustom, calls=%fused_computation.151 | custom fusion | bytes 12292 | tf_op jit(solution)/shard_map/scatter | solution.py:106
  414.1 0.0 copy-done.2
  414.1 1.3 multiply_reduce_fusion
  415.4 1.4 pad_maximum_fusion
  416.8 14.9 %all_to_all.11 = f32[32,1,2]{2,1,0:T(1,128)S(1)} all-to-all(f32[32,1,2]{2,1,0:T(1,128)S(1)} %broadcast_in_dim.24), channel_id=1, replica_groups=mesh['seq_0'=8,'seq_1'=4,'vocab_0'=4,'vocab_1'=2] {'seq_0','seq_1'}, dimensions={0} | all-to-all | bytes 512 | tf_op jit(solution)/shard_map/all_to_all | solution.py:48
  431.7 0.1 reduce_sum.49
  431.7 0.6 fusion.83
  (8 shorter events, 0.2 us)
Async XLA Ops:
  7.2 61.7 %all-gather.10.cloned.1.call-start = ((), (), s32[]{:S(2)}) async-start(), calls=%async_computation.2 | async-start | bytes 3538944 | tf_op jit(solution)/shard_map/all_gather | solution.py:16
  79.7 7.5 %copy-start.1 = (s32[3072]{0:T(1024)S(1)}, s32[3072]{0:T(1024)}, u32[]{:S(2)}) copy-start(s32[3072]{0:T(1024)} %param.7) | copy-start | bytes 36868
  79.7 247.3 %copy-start = (s32[3072]{0:T(1024)S(1)}, s32[3072]{0:T(1024)}, u32[]{:S(2)}) copy-start(s32[3072]{0:T(1024)} %param.8) | copy-start | bytes 36868
  79.7 247.3 %all-to-all-start = ((bf16[8,3072,448]{1,2,0:T(8,128)(2,1)}), bf16[8,3072,448]{1,2,0:T(8,128)(2,1)}, u32[]{:S(2)}, u32[]{:S(2)}) async-start(bf16[8,3072,448]{1,2,0:T(8,128)(2,1)} %stack.2), calls=%async_computation | async-start | bytes 44040192 | tf_op jit(solution)/shard_map/all_to_all | solution.py:97
  345.8 68.3 %copy-start.2 = (s32[96]{0:T(128)S(1)}, s32[96]{0:T(128)}, u32[]{:S(2)}) copy-start(s32[96]{0:T(128)} %param.9) | copy-start | bytes 1156
Sparse Core Ops, SparseCore 0:
  20.4 48.4 all-gather.9
